TPU v7x, 32 devices: a whole 2x2x4 slice. The times are simulated.
32 devices in a mesh: dp: 8 (over z, x), mp: 4 (over y, core).
Axes of the slice: x: 2, y: 2, z: 4, core: 2. Of those that a mesh axis runs over, the one named last changes fastest.
Arguments:
- hidden: bfloat16 [8, 512, 4608], P('dp', 'mp'), may hold values from -6 to 6
- lengths: int32 [8], P('dp'), may hold values from 64 to 512
- norm_gain: float32 [4608], replicated, may hold values from 0.25 to 1.75
- w_query: bfloat16 [4608, 2048], P('dp', 'mp'), may hold values from -0.09375 to 0.09375
- w_key: bfloat16 [4608, 1024], P('dp', 'mp'), may hold values from -0.09375 to 0.09375
- w_value: bfloat16 [4608, 1024], P('dp', 'mp'), may hold values from -0.09375 to 0.09375
- w_out: bfloat16 [2048, 4608], P('mp', 'dp'), may hold values from -0.125 to 0.125
- post_gain: float32 [4608], replicated, may hold values from 0.25 to 1.75
Outputs:
- mixed: bfloat16 [8, 512, 4608], P('dp', 'mp')
- key_cache: bfloat16 [8, 512, 1024], P('dp', None, 'mp')
- value_cache: bfloat16 [8, 512, 1024], P('dp', None, 'mp')
All inputs are finite; a program needn't handle non-finite values.
Results may differ from a plain program's by a relative error of at most 0.01.
Values may be sent and summed in bfloat16 or wider, within the bound.
A program may use at most 128 MiB of HBM per device.

v0:
```python
import jax
import jax.numpy as jnp
from jax import lax
from jax.sharding import PartitionSpec as P

HD = 128


def rotate(values, positions):
    half = values.shape[-1] // 2
    freqs = 10000.0 ** (-jnp.arange(half, dtype=jnp.float32) / half)
    angles = positions.astype(jnp.float32)[:, None] * freqs[None, :]
    cosine = jnp.cos(angles)[:, None, :]
    sine = jnp.sin(angles)[:, None, :]
    first = values[..., :half]
    second = values[..., half:]
    return jnp.concatenate(
        [first * cosine - second * sine, second * cosine + first * sine], axis=-1
    )


def attend(query_rows, key_rows, value_rows, row_index, length):
    score = jnp.einsum("qkgd,tkd->kgqt", query_rows, key_rows, preferred_element_type=jnp.float32)
    score = 50.0 * jnp.tanh(score / 50.0)
    key_index = jnp.arange(key_rows.shape[0], dtype=jnp.int32)
    keep = (key_index[None, :] <= row_index[:, None]) & (key_index[None, :] < length)
    score = jnp.where(keep[None, None], score, -1e30)
    top = jnp.max(score, axis=-1, keepdims=True)
    expo = jnp.exp(score - top)
    weights = (expo / jnp.sum(expo, axis=-1, keepdims=True)).astype(jnp.bfloat16)
    return jnp.einsum(
        "kgqt,tkd->qkgd", weights, value_rows, preferred_element_type=jnp.float32
    ).astype(jnp.bfloat16)


def local(hidden, lengths, norm_gain, w_query, w_key, w_value, w_out, post_gain):
    rollouts, local_len, width = hidden.shape
    maxlen = local_len * lax.axis_size("mp")
    q_heads = w_query.shape[1] // HD
    kv_heads = w_key.shape[1] // HD
    group = q_heads // kv_heads
    rows_f = hidden.astype(jnp.float32)
    normed = (
        rows_f * lax.rsqrt(jnp.mean(rows_f * rows_f, axis=-1, keepdims=True) + 1e-06) * norm_gain
    ).astype(jnp.bfloat16)
    gathered = lax.all_gather(normed, "mp", axis=1, tiled=True)
    flat = gathered.reshape(rollouts * maxlen, width)
    pieces = (
        lax.all_gather(w_query, "dp", axis=0, tiled=True),
        lax.all_gather(w_key, "dp", axis=0, tiled=True),
        lax.all_gather(w_value, "dp", axis=0, tiled=True),
    )
    qraw, kraw, vraw = tuple(
        (jnp.dot(flat, piece, preferred_element_type=jnp.float32) for piece in pieces)
    )
    positions = jnp.arange(maxlen, dtype=jnp.int32)
    query = (
        rotate(qraw.reshape(rollouts, maxlen, q_heads, HD), positions) * 144.0 ** (-0.5)
    ).astype(jnp.bfloat16)
    key = rotate(kraw.reshape(rollouts, maxlen, kv_heads, HD), positions).astype(jnp.bfloat16)
    value = vraw.reshape(rollouts, maxlen, kv_heads, HD).astype(jnp.bfloat16)
    grouped = query.reshape(rollouts, maxlen, kv_heads, group, HD)
    length = lengths[0]
    outputs = [attend(grouped[0], key[0], value[0], positions, length)]
    attended = jnp.stack(outputs).reshape(rollouts * maxlen, q_heads * HD)
    partial_value = (
        jnp.dot(
            attended,
            lax.all_gather(w_out, "dp", axis=1, tiled=True),
            preferred_element_type=jnp.float32,
        )
        .astype(jnp.bfloat16)
        .astype(jnp.float32)
    )
    projected = lax.psum_scatter(
        partial_value.reshape(rollouts, maxlen, width).astype(jnp.bfloat16),
        "mp",
        scatter_dimension=1,
        tiled=True,
    ).astype(jnp.float32)
    post = (
        projected
        * lax.rsqrt(jnp.mean(projected * projected, axis=-1, keepdims=True) + 1e-06)
        * post_gain
    )
    own_rows = lax.axis_index("mp") * local_len + jnp.arange(local_len, dtype=jnp.int32)
    live_local = (own_rows[None, :] < lengths[:, None])[:, :, None]
    mixed = jnp.where(live_local, rows_f + post, 0.0).astype(jnp.bfloat16)
    live_all = (positions[None, :] < lengths[:, None])[:, :, None]
    key_cache = jnp.where(
        live_all, key.reshape(rollouts, maxlen, kv_heads * HD), jnp.zeros((), jnp.bfloat16)
    )
    value_cache = jnp.where(
        live_all, value.reshape(rollouts, maxlen, kv_heads * HD), jnp.zeros((), jnp.bfloat16)
    )
    return (mixed, key_cache, value_cache)


def solution(mesh):
    return jax.shard_map(
        local,
        mesh=mesh,
        in_specs=(
            P("dp", "mp", None),
            P("dp"),
            P(),
            P("dp", "mp"),
            P("dp", "mp"),
            P("dp", "mp"),
            P("mp", "dp"),
            P(),
        ),
        out_specs=(P("dp", "mp", None), P("dp", None, "mp"), P("dp", None, "mp")),
        check_vma=False,
    )
```

profile of v0, /device:TPU:0, one launch (start us, length us, event | category | flops | bytes accessed | tf_op | source)
XLA Modules:
  0.0 381.2 jit_solution(8354099245536206741)
XLA Ops:
  7.2 0.0 all-gather.10.cloned.1.call-start
  7.2 0.7 all-gather.10.cloned.1.call-update
  7.9 0.0 all-gather.8.cloned.1.call-start
  7.9 0.7 all-gather.8.cloned.1.call-update
  8.6 0.0 all-gather.6.cloned.1.call-start
  8.7 1.6 fusion.11
  10.3 2.6 fusion.13
  12.9 0.0 all-gather.6.cloned.1.call-update
  12.9 0.0 all-gather.12.cloned.1.call-start
  13.0 0.5 all-gather.12.cloned.1.call-update
  13.5 0.0 all-gather.14.cloned.1.call-start
  13.6 0.5 all-gather.14.cloned.1.call-update
  14.1 0.0 reduce-scatter.2.cloned.1.call-start
  14.8 0.8 fusion.32
  15.7 0.5 multiply_cosine_fusion
  16.2 48.5 %all-gather.10.cloned.1.call-done = bf16[4608,256]{1,0:T(8,128)(2,1)} async-done(((bf16[576,256]{1,0:T(8,128)(2,1)}), bf16[4608,256]{1,0:T(8,128)(2,1)}) %all-gather.10.cloned.1.call-update) | async-done | bytes 2359312 | tf_op jit(solution)/shard_map/all_gather | solution.py:50
  64.7 4.3 %copy.12 = bf16[256,4608]{1,0:T(8,128)(2,1)} copy(bf16[256,4608]{0,1:T(8,128)(2,1)} %bitcast.78) | data formatting | bytes 4718592 | tf_op jit(solution)/shard_map/dot_general | solution.py:54
  69.0 48.2 %all-gather.8.cloned.1.call-done = bf16[4608,256]{1,0:T(8,128)(2,1)} async-done(((bf16[576,256]{1,0:T(8,128)(2,1)}), bf16[4608,256]{1,0:T(8,128)(2,1)}) %all-gather.8.cloned.1.call-update) | async-done | bytes 2359312 | tf_op jit(solution)/shard_map/all_gather | solution.py:51
  117.3 2.8 copy.11
  120.1 35.3 %all-gather.6.cloned.1.call-done = bf16[1,512,4608]{2,1,0:T(8,128)(2,1)} async-done(((bf16[1,128,4608]{2,1,0:T(8,128)(2,1)}), bf16[1,512,4608]{2,1,0:T(8,128)(2,1)}) %all-gather.6.cloned.1.call-update) | async-done | bytes 4718608 | tf_op jit(solution)/shard_map/all_gather | solution.py:46
  155.4 0.0 copy-start.3
  155.4 4.6 %fusion.25 = f32[1,512,2,128]{1,3,2,0:T(8,128)S(1)} fusion(bf16[2,128,4608]{2,1,0:T(8,128)(2,1)} %bitcast.81, bf16[1,512,4608]{2,1,0:T(8,128)(2,1)} %all-gather.6.cloned.1.call-done), kind=kOutput, calls=%fused_computation.32 | convolution fusion | flops 1207959552 | bytes 7602176 | tf_op jit(solution)/shard_map/dot_general | solution.py:54
  160.1 0.1 subtract_convert_fusion
  160.2 0.0 copy-done.3
  160.2 1.4 fusion.28
  161.6 75.2 %all-gather.12.cloned.1.call-done = bf16[4608,512]{1,0:T(8,128)(2,1)} async-done(((bf16[576,512]{1,0:T(8,128)(2,1)}), bf16[4608,512]{1,0:T(8,128)(2,1)}) %all-gather.12.cloned.1.call-update) | async-done | bytes 4718608 | tf_op jit(solution)/shard_map/all_gather | solution.py:49
  236.8 6.7 %copy.13 = bf16[512,4608]{1,0:T(8,128)(2,1)} copy(bf16[512,4608]{0,1:T(8,128)(2,1)} %bitcast.76) | data formatting | bytes 9437184 | tf_op jit(solution)/shard_map/dot_general | solution.py:54
  243.5 6.4 %fusion.21 = f32[1,512,4,128]{1,3,2,0:T(8,128)S(1)} fusion(bf16[4,128,4608]{2,1,0:T(8,128)(2,1)} %bitcast.77, bf16[1,512,4608]{2,1,0:T(8,128)(2,1)} %all-gather.6.cloned.1.call-done), kind=kOutput, calls=%fused_computation.30 | convolution fusion | flops 2415919104 | bytes 10485760 | tf_op jit(solution)/shard_map/dot_general | solution.py:54
  249.9 0.2 multiply_subtract_fusion
  250.1 0.0 copy-start.1
  250.1 0.3 copy.15
  250.4 0.3 copy.14
  250.8 0.3 fusion.31
  251.1 0.0 copy-done.1
  251.2 1.9 fusion.53
  253.1 2.4 fusion.24
  255.5 61.1 %all-gather.14.cloned.1.call-done = bf16[512,4608]{0,1:T(8,128)(2,1)} async-done(((bf16[512,576]{0,1:T(8,128)(2,1)}), bf16[512,4608]{0,1:T(8,128)(2,1)}) %all-gather.14.cloned.1.call-update) | async-done | bytes 4718608 | tf_op jit(solution)/shard_map/all_gather | solution.py:69
  316.6 6.7 %fusion.1 = bf16[1,512,4608]{2,1,0:T(8,128)(2,1)} fusion(bf16[512,512]{0,1:T(8,128)(2,1)S(1)} %bitcast.90, bf16[512,4608]{0,1:T(8,128)(2,1)} %all-gather.14.cloned.1.call-done), kind=kOutput, calls=%fused_computation.2 | convolution fusion | flops 2418278400 | bytes 9961472 | tf_op jit(solution)/shard_map/dot_general | solution.py:67
  323.3 0.0 copy-start
  323.3 0.0 copy-start.2
  323.3 0.0 reduce-scatter.2.cloned.1.call-update
  323.4 0.1 copy.19
  323.5 0.1 copy.18
  323.7 0.9 broadcast_select_fusion
  324.6 45.2 %reduce-scatter.2.cloned.1.call-done = bf16[1,128,4608]{2,1,0:T(8,128)(2,1)} async-done(((bf16[1,512,4608]{2,1,0:T(8,128)(2,1)}), bf16[1,128,4608]{2,1,0:T(8,128)(2,1)}) %reduce-scatter.2.cloned.1.call-update) | async-done | bytes 1179664 | tf_op jit(solution)/shard_map/reduce_scatter | solution.py:75
  369.8 1.6 fusion.9
  371.4 0.0 copy-done
  371.4 0.0 copy-done.2
  371.4 2.9 fusion.15
  (7 shorter events, 0.1 us)
Async XLA Ops:
  7.2 57.6 %all-gather.10.cloned.1.call-start = ((), (), s32[]{:S(2)}) async-start(), calls=%async_computation.3 | async-start | bytes 2654208 | tf_op jit(solution)/shard_map/all_gather | solution.py:50
  7.9 109.4 %all-gather.8.cloned.1.call-start = ((), (), s32[]{:S(2)}) async-start(), calls=%async_computation.2 | async-start | bytes 2654208 | tf_op jit(solution)/shard_map/all_gather | solution.py:51
  8.6 146.8 %all-gather.6.cloned.1.call-start = ((), (), s32[]{:S(2)}) async-start(), calls=%async_computation.1 | async-start | bytes 5898240 | tf_op jit(solution)/shard_map/all_gather | solution.py:46
  12.9 223.9 %all-gather.12.cloned.1.call-start = ((), (), s32[]{:S(2)}) async-start(), calls=%async_computation.4 | async-start | bytes 5308416 | tf_op jit(solution)/shard_map/all_gather | solution.py:49
  13.5 303.1 %all-gather.14.cloned.1.call-start = ((), (), s32[]{:S(2)}) async-start(), calls=%async_computation.5 | async-start | bytes 5308416 | tf_op jit(solution)/shard_map/all_gather | solution.py:69
  14.1 355.7 %reduce-scatter.2.cloned.1.call-start = ((), (), s32[]{:S(2)}) async-start(), calls=%async_computation.6 | async-start | bytes 5898240 | tf_op jit(solution)/shard_map/reduce_scatter | solution.py:75
  155.4 4.7 %copy-start.3 = (bf16[1,512,4608]{2,1,0:T(8,128)(2,1)S(1)}, bf16[1,512,4608]{2,1,0:T(8,128)(2,1)}, u32[]{:S(2)}) copy-start(bf16[1,512,4608]{2,1,0:T(8,128)(2,1)} %all-gather.6.cloned.1.call-done) | copy-start | bytes 14155780
  250.1 1.0 copy-start.1
  323.3 48.1 %copy-start = (bf16[1,128,4608]{2,1,0:T(8,128)(2,1)S(1)}, bf16[1,128,4608]{2,1,0:T(8,128)(2,1)}, u32[]{:S(2)}) copy-start(bf16[1,128,4608]{2,1,0:T(8,128)(2,1)} %param.8) | copy-start | bytes 3538948
  323.3 48.1 %copy-start.2 = (f32[4608]{0:T(1024)S(1)}, f32[4608]{0:T(1024)}, u32[]{:S(2)}) copy-start(f32[4608]{0:T(1024)} %param.15) | copy-start | bytes 55300
Sparse Core Ops, SparseCore 0:
  10.2 54.5 all-gather.9
  66.9 50.3 all-gather.7
  119.4 35.9 all-gather.5
  157.5 79.3 all-gather.11
  238.9 77.6 all-gather.13
  323.5 46.3 reduce-scatter.1
where the time goes:
time: 382 us; the launch traced here: 381 us
  waiting for transfers between devices  316 us (83%)
  matrix products  23.5 us (6%)
  between operations  14.9 us (4%)
  local copies, waits for them, and re-layouts  14.8 us (4%)
  other arithmetic  11.6 us (3%)
    all_gather x1, waiting for transfers between devices, local(): lax.all_gather(w_query, 'dp', axis=0, tiled=True)  75.2 us
    all_gather x1, waiting for transfers between devices, local(): lax.all_gather(w_out, 'dp', axis=1, tiled=True)  61.1 us
    all_gather x1, waiting for transfers between devices, local(): lax.all_gather(w_key, 'dp', axis=0, tiled=True)  48.5 us
    all_gather x1, waiting for transfers between devices, local(): lax.all_gather(w_value, 'dp', axis=0, tiled=True)  48.2 us
    reduce_scatter x1, waiting for transfers between devices, local(): lax.psum_scatter(partial_value.reshape(rollouts, maxlen, width).astype(jn...  45.2 us
    all_gather x1, waiting for transfers between devices, local(): gathered = lax.all_gather(normed, 'mp', axis=1, tiled=True)  35.3 us
    dot_general x3, local copies, waits for them, and re-layouts, local(): jnp.dot(flat, piece, preferred_element_type=jnp.float32)  13.9 us
    dot_general x3, matrix products, local(): jnp.dot(flat, piece, preferred_element_type=jnp.float32)  12.4 us
  transfers between devices with their start and end apart: 6, of which 6 were waited for; matrix products, arithmetic and copies ran while one was open for 10% of the time, Pallas kernels for 0%

commit v1 on v0

--- a/solution.py
+++ b/solution.py
@@ -43,7 +43,12 @@
     normed = (
         rows_f * lax.rsqrt(jnp.mean(rows_f * rows_f, axis=-1, keepdims=True) + 1e-06) * norm_gain
     ).astype(jnp.bfloat16)
-    gathered = lax.all_gather(normed, "mp", axis=1, tiled=True)
+    ring = [normed]
+    for hop in range(3):
+        ring.append(lax.ppermute(ring[-1], "mp", [(dev, (dev + 1) % 4) for dev in range(4)]))
+    gathered = jnp.roll(
+        jnp.concatenate(ring[::-1], axis=1), (lax.axis_index("mp") + 1) * ring[0].shape[1], axis=1
+    )
     flat = gathered.reshape(rollouts * maxlen, width)
     pieces = (
         lax.all_gather(w_query, "dp", axis=0, tiled=True),

time: 382 us -> 342 us (0.90)
  waiting for transfers between devices: 316 us -> 255 us
  local copies, waits for them, and re-layouts: 14.8 us -> 25.1 us
  matrix products: 23.5 us -> 29 us
  other arithmetic: 11.6 us -> 16.5 us
    all_gather x1, waiting for transfers between devices: 48.5 us -> 0.01 us  [local(): lax.all_gather(w_key, 'dp', axis=0, tiled=True)]
    ppermute x0 -> x3, waiting for transfers between devices: none -> 44.3 us  [local(): lax.ppermute(ring[-1], 'mp', [(dev, (dev + 1) % 4) for dev in range(4)])]
    all_gather x1 -> x0, waiting for transfers between devices: 35.3 us -> none  [local(): gathered = lax.all_gather(normed, 'mp', axis=1, tiled=True)]
    unnamed x8 -> x28, local copies, waits for them, and re-layouts: 0.02 us -> 9.26 us
    all_gather x1, waiting for transfers between devices: 75.2 us -> 67.1 us  [local(): lax.all_gather(w_query, 'dp', axis=0, tiled=True)]
    all_gather x1, waiting for transfers between devices: 48.2 us -> 40.3 us  [local(): lax.all_gather(w_value, 'dp', axis=0, tiled=True)]
    all_gather x1, waiting for transfers between devices: 61.1 us -> 56.1 us  [local(): lax.all_gather(w_out, 'dp', axis=1, tiled=True)]
  transfers between devices with their start and end apart: 6 -> 8, of which waited for: 6 -> 7; matrix products, arithmetic and copies ran while one was open for 10% -> 17% of each run, Pallas kernels for 0% -> 0%
where the time goes in v1:
time: 342 us; the launch traced here: 341 us
  waiting for transfers between devices  255 us (75%)
  matrix products  29 us (8%)
  local copies, waits for them, and re-layouts  25.1 us (7%)
  other arithmetic  16.5 us (5%)
  between operations  14.7 us (4%)
    all_gather x1, waiting for transfers between devices, local(): lax.all_gather(w_query, 'dp', axis=0, tiled=True)  67.1 us
    all_gather x1, waiting for transfers between devices, local(): lax.all_gather(w_out, 'dp', axis=1, tiled=True)  56.1 us
    reduce_scatter x1, waiting for transfers between devices, local(): lax.psum_scatter(partial_value.reshape(rollouts, maxlen, width).astype(jn...  45.2 us
    ppermute x3, waiting for transfers between devices, local(): lax.ppermute(ring[-1], 'mp', [(dev, (dev + 1) % 4) for dev in range(4)])  44.3 us
    all_gather x1, waiting for transfers between devices, local(): lax.all_gather(w_value, 'dp', axis=0, tiled=True)  40.3 us
    dot_general x3, matrix products, local(): jnp.dot(flat, piece, preferred_element_type=jnp.float32)  15.8 us
    dot_general x3, local copies, waits for them, and re-layouts, local(): jnp.dot(flat, piece, preferred_element_type=jnp.float32)  13.8 us
    unnamed x28, local copies, waits for them, and re-layouts  9.26 us
  transfers between devices with their start and end apart: 8, of which 7 were waited for; matrix products, arithmetic and copies ran while one was open for 17% of the time, Pallas kernels for 0%

profile of v1, /device:TPU:0, one launch (start us, length us, event | category | flops | bytes accessed | tf_op | source)
XLA Modules:
  0.0 341.2 jit_solution(10807734696642469752)
XLA Ops:
  7.2 0.0 all-gather.7.cloned.1.call-start
  7.2 0.7 all-gather.7.cloned.1.call-update
  7.9 0.0 all-gather.5.cloned.1.call-start
  7.9 0.7 all-gather.5.cloned.1.call-update
  8.6 0.0 all-gather.9.cloned.1.call-start
  8.7 0.7 all-gather.9.cloned.1.call-update
  9.4 0.0 all-gather.11.cloned.1.call-start
  9.4 1.6 fusion.14
  11.0 1.6 fusion.16
  12.6 0.0 copy-start
  12.7 0.5 collective-permute-start
  13.2 15.8 %collective-permute-done = bf16[1,128,4608]{2,1,0:T(8,128)(2,1)S(1)} collective-permute-done((bf16[1,128,4608]{2,1,0:T(8,128)(2,1)S(1)}, bf16[1,128,4608]{2,1,0:T(8,128)(2,1)S(1)}, u32[]{:S(2)}, u32[]{:S(2)}) %collective-permute-start) | collective-permute-done | bytes 1179680 | tf_op jit(solution)/shard_map/ppermute | solution.py:48
  29.0 0.0 collective-permute-start.1
  29.0 15.6 %collective-permute-done.1 = bf16[1,128,4608]{2,1,0:T(8,128)(2,1)S(1)} collective-permute-done((bf16[1,128,4608]{2,1,0:T(8,128)(2,1)S(1)}, bf16[1,128,4608]{2,1,0:T(8,128)(2,1)S(1)}, u32[]{:S(2)}, u32[]{:S(2)}) %collective-permute-start.1) | collective-permute-done | bytes 1179680 | tf_op jit(solution)/shard_map/ppermute | solution.py:48
  44.7 0.0 collective-permute-start.2
  44.7 0.0 all-gather.11.cloned.1.call-update
  44.7 0.0 reduce-scatter.2.cloned.1.call-start
  45.4 0.0 copy-start.9
  45.5 0.8 fusion.35
  46.3 1.2 multiply_cosine_fusion
  47.5 12.9 %collective-permute-done.2 = bf16[1,128,4608]{2,1,0:T(8,128)(2,1)} collective-permute-done((bf16[1,128,4608]{2,1,0:T(8,128)(2,1)S(1)}, bf16[1,128,4608]{2,1,0:T(8,128)(2,1)}, u32[]{:S(2)}, u32[]{:S(2)}) %collective-permute-start.2) | collective-permute-done | bytes 1179680 | tf_op jit(solution)/shard_map/ppermute | solution.py:48
  60.4 2.4 constant_dynamic-update-slice_fusion.7
  62.8 1.1 constant_dynamic-update-slice_fusion.6
  63.9 1.1 constant_dynamic-update-slice_fusion.5
  65.0 0.0 copy-done
  65.0 0.0 copy-done.9
  65.0 1.4 constant_dynamic-update-slice_fusion.4
  66.3 2.4 constant_dynamic-update-slice_fusion.3
  68.7 1.1 constant_dynamic-update-slice_fusion.2
  69.9 1.1 constant_dynamic-update-slice_fusion.1
  71.0 1.4 constant_dynamic-update-slice_fusion
  72.4 4.3 %copy.12 = bf16[256,4608]{1,0:T(8,128)(2,1)} copy(bf16[256,4608]{0,1:T(8,128)(2,1)} %bitcast.78) | data formatting | bytes 4718592 | tf_op jit(solution)/shard_map/dot_general | solution.py:59
  76.8 40.3 %all-gather.5.cloned.1.call-done = bf16[4608,256]{1,0:T(8,128)(2,1)} async-done(((bf16[576,256]{1,0:T(8,128)(2,1)}), bf16[4608,256]{1,0:T(8,128)(2,1)}) %all-gather.5.cloned.1.call-update) | async-done | bytes 2359312 | tf_op jit(solution)/shard_map/all_gather | solution.py:56
  117.1 2.8 copy.11
  119.9 0.0 copy-start.1
  120.0 0.0 copy-start.3
  120.0 4.5 %fusion.28 = f32[1,512,2,128]{1,3,2,0:T(8,128)S(1)} fusion(bf16[2,128,4608]{2,1,0:T(8,128)(2,1)} %bitcast.81, bf16[1,1024,4608]{2,1,0:T(8,128)(2,1)} %constant_dynamic-update-slice_fusion, s32[]{:T(128)S(6)} %select_n.45), kind=kOutput, calls=%fused_computation.35 | convolution fusion | flops 1207959552 | bytes 7602180 | tf_op jit(solution)/shard_map/dot_general | solution.py:59
  124.5 0.0 copy-done.1
  124.5 0.0 copy-done.3
  124.5 0.8 subtract_convert_fusion
  125.3 4.8 %fusion.31 = bf16[512,2,128]{0,2,1:T(8,128)(2,1)} fusion(bf16[2,128,4608]{2,1,0:T(8,128)(2,1)S(1)} %bitcast.80, bf16[1,1024,4608]{2,1,0:T(8,128)(2,1)} %constant_dynamic-update-slice_fusion, s32[]{:T(128)S(6)} %select_n.45), kind=kOutput, calls=%fused_computation.36 | convolution fusion | flops 1208090624 | bytes 7340036 | tf_op jit(solution)/shard_map/dot_general | solution.py:59
  130.1 67.1 %all-gather.9.cloned.1.call-done = bf16[4608,512]{1,0:T(8,128)(2,1)} async-done(((bf16[576,512]{1,0:T(8,128)(2,1)}), bf16[4608,512]{1,0:T(8,128)(2,1)}) %all-gather.9.cloned.1.call-update) | async-done | bytes 4718608 | tf_op jit(solution)/shard_map/all_gather | solution.py:54
  197.2 6.7 %copy.13 = bf16[512,4608]{1,0:T(8,128)(2,1)} copy(bf16[512,4608]{0,1:T(8,128)(2,1)} %bitcast.76) | data formatting | bytes 9437184 | tf_op jit(solution)/shard_map/dot_general | solution.py:59
  203.9 6.5 %fusion.24 = f32[1,512,4,128]{1,3,2,0:T(8,128)S(1)} fusion(bf16[4,128,4608]{2,1,0:T(8,128)(2,1)} %bitcast.77, bf16[1,1024,4608]{2,1,0:T(8,128)(2,1)} %constant_dynamic-update-slice_fusion, s32[]{:T(128)S(6)} %select_n.45), kind=kOutput, calls=%fused_computation.33 | convolution fusion | flops 2415919104 | bytes 10485764 | tf_op jit(solution)/shard_map/dot_general | solution.py:59
  210.4 0.0 copy-done.2
  210.4 0.0 copy-done.4
  210.4 0.0 copy-start.6
  210.5 0.0 copy-start.7
  210.5 1.0 multiply_subtract_fusion
  211.5 0.3 copy.14
  211.8 1.4 copy.15
  213.2 1.1 fusion.34
  214.3 0.0 copy-done.6
  214.3 3.1 fusion.59
  217.5 3.4 fusion.27
  220.9 56.1 %all-gather.11.cloned.1.call-done = bf16[512,4608]{0,1:T(8,128)(2,1)} async-done(((bf16[512,576]{0,1:T(8,128)(2,1)}), bf16[512,4608]{0,1:T(8,128)(2,1)}) %all-gather.11.cloned.1.call-update) | async-done | bytes 4718608 | tf_op jit(solution)/shard_map/all_gather | solution.py:74
  277.0 6.7 %fusion.1 = bf16[1,512,4608]{2,1,0:T(8,128)(2,1)} fusion(bf16[512,512]{0,1:T(8,128)(2,1)S(1)} %bitcast.90, bf16[512,4608]{0,1:T(8,128)(2,1)} %all-gather.11.cloned.1.call-done), kind=kOutput, calls=%fused_computation.2 | convolution fusion | flops 2418278400 | bytes 9961472 | tf_op jit(solution)/shard_map/dot_general | solution.py:72
  283.7 0.0 reduce-scatter.2.cloned.1.call-update
  283.7 0.1 copy.18
  283.9 0.1 copy.19
  284.0 0.9 broadcast_select_fusion
  284.9 45.2 %reduce-scatter.2.cloned.1.call-done = bf16[1,128,4608]{2,1,0:T(8,128)(2,1)} async-done(((bf16[1,512,4608]{2,1,0:T(8,128)(2,1)}), bf16[1,128,4608]{2,1,0:T(8,128)(2,1)}) %reduce-scatter.2.cloned.1.call-update) | async-done | bytes 1179664 | tf_op jit(solution)/shard_map/reduce_scatter | solution.py:80
  330.2 1.6 fusion.12
  331.8 2.9 fusion.18
  (17 shorter events, 0.1 us)
Async XLA Ops:
  7.2 65.3 %all-gather.7.cloned.1.call-start = ((), (), s32[]{:S(2)}) async-start(), calls=%async_computation.2 | async-start | bytes 2654208 | tf_op jit(solution)/shard_map/all_gather | solution.py:55
  7.9 109.2 %all-gather.5.cloned.1.call-start = ((), (), s32[]{:S(2)}) async-start(), calls=%async_computation.1 | async-start | bytes 2654208 | tf_op jit(solution)/shard_map/all_gather | solution.py:56
  8.6 188.6 %all-gather.9.cloned.1.call-start = ((), (), s32[]{:S(2)}) async-start(), calls=%async_computation.3 | async-start | bytes 5308416 | tf_op jit(solution)/shard_map/all_gather | solution.py:54
  9.4 267.6 %all-gather.11.cloned.1.call-start = ((), (), s32[]{:S(2)}) async-start(), calls=%async_computation.4 | async-start | bytes 5308416 | tf_op jit(solution)/shard_map/all_gather | solution.py:74
  12.6 52.3 %copy-start = (bf16[1,128,4608]{2,1,0:T(8,128)(2,1)S(1)}, bf16[1,128,4608]{2,1,0:T(8,128)(2,1)}, u32[]{:S(2)}) copy-start(bf16[1,128,4608]{2,1,0:T(8,128)(2,1)} %param.8) | copy-start | bytes 3538948
  12.7 16.4 %collective-permute-start = (bf16[1,128,4608]{2,1,0:T(8,128)(2,1)S(1)}, bf16[1,128,4608]{2,1,0:T(8,128)(2,1)S(1)}, u32[]{:S(2)}, u32[]{:S(2)}) collective-permute-start(bf16[1,128,4608]{2,1,0:T(8,128)(2,1)S(1)} %fusion.16), channel_id=1, source_target_pairs={{0,1},{1,2},{2,3},{3,0},{4,5},{5,6},{6,7},{7,4},{8,9},{9,10},{10,1... | collective-permute-start | bytes 3538952 | tf_op jit(solution)/shard_map/ppermute | solution.py:48
  29.0 15.6 %collective-permute-start.1 = (bf16[1,128,4608]{2,1,0:T(8,128)(2,1)S(1)}, bf16[1,128,4608]{2,1,0:T(8,128)(2,1)S(1)}, u32[]{:S(2)}, u32[]{:S(2)}) collective-permute-start(bf16[1,128,4608]{2,1,0:T(8,128)(2,1)S(1)} %collective-permute-done), channel_id=1, source_target_pairs={{0,1},{1,2},{2,3},{3,0},{4,5},{5,6},{6,7},{7,4},{8,9},{9,10},{10,1... | collective-permute-start | bytes 3538952 | tf_op jit(solution)/shard_map/ppermute | solution.py:48
  44.7 15.7 %collective-permute-start.2 = (bf16[1,128,4608]{2,1,0:T(8,128)(2,1)S(1)}, bf16[1,128,4608]{2,1,0:T(8,128)(2,1)}, u32[]{:S(2)}, u32[]{:S(2)}) collective-permute-start(bf16[1,128,4608]{2,1,0:T(8,128)(2,1)S(1)} %collective-permute-done.1), channel_id=1, source_target_pairs={{0,1},{1,2},{2,3},{3,0},{4,5},{5,6},{6,7},{7,4},{8,9},{9,10},{10,1... | collective-permute-start | bytes 3538952 | tf_op jit(solution)/shard_map/ppermute | solution.py:48
  44.7 285.5 %reduce-scatter.2.cloned.1.call-start = ((), (), s32[]{:S(2)}) async-start(), calls=%async_computation.5 | async-start | bytes 5898240 | tf_op jit(solution)/shard_map/reduce_scatter | solution.py:80
  45.4 19.6 %copy-start.9 = (f32[4608]{0:T(1024)S(1)}, f32[4608]{0:T(1024)}, u32[]{:S(2)}) copy-start(f32[4608]{0:T(1024)} %param.10) | copy-start | bytes 55300
  119.9 4.6 %copy-start.1 = (f32[512,64]{0,1:T(8,128)S(1)}, f32[512,64]{0,1:T(8,128)}, u32[]{:S(2)}) copy-start(f32[512,64]{0,1:T(8,128)} %get-tuple-element.7) | copy-start | bytes 393220
  120.0 4.6 %copy-start.3 = (f32[512,64]{0,1:T(8,128)S(1)}, f32[512,64]{0,1:T(8,128)}, u32[]{:S(2)}) copy-start(f32[512,64]{0,1:T(8,128)} %get-tuple-element.8) | copy-start | bytes 393220
  203.9 6.5 %copy-start.2 = (f32[512,64]{0,1:T(8,128)S(1)}, f32[512,64]{0,1:T(8,128)}, u32[]{:S(2)}) copy-start(f32[512,64]{0,1:T(8,128)} %get-tuple-element.7) | copy-start | bytes 393220
  203.9 6.5 %copy-start.4 = (f32[512,64]{0,1:T(8,128)S(1)}, f32[512,64]{0,1:T(8,128)}, u32[]{:S(2)}) copy-start(f32[512,64]{0,1:T(8,128)} %get-tuple-element.8) | copy-start | bytes 393220
  210.4 3.9 %copy-start.6 = (bf16[1,512,2,64]{1,3,2,0:T(8,128)(2,1)S(1)}, bf16[1,512,2,64]{1,3,2,0:T(8,128)(2,1)}, u32[]{:S(2)}) copy-start(bf16[1,512,2,64]{1,3,2,0:T(8,128)(2,1)} %get-tuple-element.5) | copy-start | bytes 393220
  210.5 3.9 %copy-start.7 = (bf16[1,512,2,64]{1,3,2,0:T(8,128)(2,1)S(1)}, bf16[1,512,2,64]{1,3,2,0:T(8,128)(2,1)}, u32[]{:S(2)}) copy-start(bf16[1,512,2,64]{1,3,2,0:T(8,128)(2,1)} %get-tuple-element.6) | copy-start | bytes 393220
  214.3 3.1 copy-start.5
  214.3 3.1 copy-start.8
  283.7 48.1 %copy-start.10 = (f32[4608]{0:T(1024)S(1)}, f32[4608]{0:T(1024)}, u32[]{:S(2)}) copy-start(f32[4608]{0:T(1024)} %param.15) | copy-start | bytes 55300
Sparse Core Ops, SparseCore 0:
  10.2 54.3 all-gather.6
  66.7 50.3 all-gather.4
  119.3 77.8 all-gather.8
  199.3 77.6 all-gather.10
  283.8 46.3 reduce-scatter.1
